TPU v7x, 32 devices: a 4x4x1 block of a 4x4x8 slice. The times are simulated.
32 devices in a mesh: data: 1 (over z), pp: 4 (over y), ep: 8 (over x, core).
Axes of the slice: x: 4, y: 4, z: 1, core: 2. Of those that a mesh axis runs over, the one named last changes fastest.
The devices are a block of a 4x4x8 slice.
Arguments:
- expert_out: bfloat16 [4, 1, 64, 768, 2560], P(('data', 'pp'), None, 'ep')
- expert_ids: int32 [4, 1, 8, 512, 6], P(('data', 'pp'), None, 'ep')
- slot_ids: int32 [4, 1, 8, 512, 6], P(('data', 'pp'), None, 'ep')
- gates: float32 [4, 1, 8, 512, 6], P(('data', 'pp'), None, 'ep')
- resid: bfloat16 [4, 1, 8, 512, 2560], P(('data', 'pp'), None, 'ep')
- norm_scale: float32 [4, 2560], P('pp')
- w_query: bfloat16 [4, 2560, 2560], P('pp')
- w_key: bfloat16 [4, 2560, 2560], P('pp')
- w_value: bfloat16 [4, 2560, 2560], P('pp')
- w_out: bfloat16 [4, 20, 128, 2560], P('pp')
Outputs:
- output: bfloat16 [4, 1, 8, 512, 2560], P(('data', 'pp'), None, 'ep')
All inputs are finite; a program needn't handle non-finite values.
Results may differ from a plain program's by a relative error of at most 0.0119935.
Values are sent between devices in bfloat16 or wider.
A program may use at most 768 MiB of HBM per device.

v0:
```python
import jax
import jax.numpy as jnp
from jax import lax
from jax.sharding import PartitionSpec as P

NORM_EPS = 1e-6


def take_rows(row_table, flat_ids):
    return jnp.take(row_table, flat_ids, axis=0, mode='clip')


def combine_rows(row_table, flat_ids, weights, resid):
    gathered = jax.vmap(take_rows)(row_table, flat_ids)
    mixed = jnp.sum(gathered.astype(jnp.float32) * weights[..., None], axis=3)
    return (resid.astype(jnp.float32) + mixed).astype(jnp.bfloat16)


def attend_block(arrived, gain_row, w_query, w_key, w_value, w_out):
    head_count, head_dim = w_out.shape[0], w_out.shape[1]
    seq_len = arrived.shape[2]
    x_float = arrived.astype(jnp.float32)
    inv_rms = lax.rsqrt(jnp.mean(jnp.square(x_float), axis=-1, keepdims=True) + NORM_EPS)
    normed = (x_float * inv_rms * gain_row).astype(jnp.bfloat16)
    head_shape = arrived.shape[:3] + (head_count, head_dim)

    def project(w_mat):
        return jnp.einsum('mbld,de->mble', normed, w_mat, preferred_element_type=jnp.float32).astype(jnp.bfloat16).reshape(head_shape)

    q_heads = project(w_query)
    k_heads = project(w_key)
    v_heads = project(w_value)
    scores = jnp.einsum('mbqhe,mbkhe->mbhqk', q_heads, k_heads, preferred_element_type=jnp.float32) * head_dim ** -0.5
    positions = jnp.arange(seq_len)
    causal = positions[:, None] >= positions[None, :]
    attn_prob = jax.nn.softmax(jnp.where(causal, scores, -jnp.inf), axis=-1).astype(jnp.bfloat16)
    context = jnp.einsum('mbhqk,mbkhe->mbqhe', attn_prob, v_heads, preferred_element_type=jnp.float32).astype(jnp.bfloat16)
    proj = jnp.einsum('mbqhe,hed->mbqd', context, w_out, preferred_element_type=jnp.float32).astype(jnp.bfloat16)
    return (x_float + proj.astype(jnp.float32)).astype(jnp.bfloat16)


def solution(mesh):
    stages = mesh.shape['pp']
    ep_size = mesh.shape['ep']
    shift_pairs = [(src, (src + 1) % stages) for src in range(stages)]
    token_spec = P(('data', 'pp'), None, 'ep', None, None)
    weight_spec = P('pp', None, None)

    def local_step(expert_out, expert_ids, slot_ids, gates, resid, norm_scale, w_query, w_key, w_value, w_out):
        own_out = expert_out[0]
        micro_count, local_experts, capacity, model_dim = own_out.shape
        slot_dev = capacity // ep_size
        split_view = own_out.reshape(micro_count, local_experts, ep_size, slot_dev, model_dim)
        received = lax.all_to_all(split_view, 'ep', 2, 1, tiled=True)
        row_table = received.reshape(micro_count, local_experts * ep_size * slot_dev, model_dim)
        own_slots = slot_ids[0]
        is_kept = own_slots >= 0
        slot_base = lax.axis_index('ep') * slot_dev
        flat_ids = expert_ids[0] * slot_dev + jnp.where(is_kept, own_slots - slot_base, 0)
        weights = jnp.where(is_kept, gates[0], 0.0)
        combined = combine_rows(row_table, flat_ids, weights, resid[0])
        arrived = lax.ppermute(combined, 'pp', shift_pairs)
        result = attend_block(arrived, norm_scale[0], w_query[0], w_key[0], w_value[0], w_out[0])
        return result[None]

    return jax.shard_map(local_step, mesh=mesh, in_specs=(token_spec, token_spec, token_spec, token_spec, token_spec, P('pp', None), weight_spec, weight_spec, weight_spec, P('pp', None, None, None)), out_specs=token_spec, check_vma=False)
```

profile of v0, /device:TPU:97, one launch (start us, length us, event | category | flops | bytes accessed | tf_op | source)
XLA Modules:
  0.0 675.1 jit_solution(14150711828789817818)
XLA Ops:
  0.0 21.7 %copy.37 = bf16[1,8,8,96,2560]{4,3,1,0,2:T(8,128)(2,1)} copy(bf16[1,8,8,96,2560]{4,3,2,1,0:T(8,128)(2,1)} %bitcast.83) | data formatting | bytes 62914560 | tf_op jit(solution)/shard_map/reshape;squeeze | solution.py:53
  21.7 0.0 copy-start.3
  21.7 9.0 %all-to-all-start = ((bf16[1,8,8,96,2560]{4,3,1,0,2:T(8,128)(2,1)}), bf16[1,8,8,96,2560]{4,3,1,0,2:T(8,128)(2,1)}, u32[]{:S(2)}, u32[]{:S(2)}) async-start(bf16[1,8,8,96,2560]{4,3,1,0,2:T(8,128)(2,1)} %copy.37), calls=%async_computation | async-start | bytes 62914560 | tf_op jit(solution)/shard_map/all_to_all | solution.py:54
  30.9 0.1 copy.38
  31.0 0.2 reshape.200
  31.2 0.1 copy.51
  31.4 340.2 %all-to-all-done = bf16[1,8,8,96,2560]{4,3,1,0,2:T(8,128)(2,1)} async-done(((bf16[1,8,8,96,2560]{4,3,1,0,2:T(8,128)(2,1)}), bf16[1,8,8,96,2560]{4,3,1,0,2:T(8,128)(2,1)}, u32[]{:S(2)}, u32[]{:S(2)}) %all-to-all-start) | async-done | bytes 31457312 | tf_op jit(solution)/shard_map/all_to_all | solution.py:54
  371.5 79.0 %gather_fusion = bf16[3072,2560]{1,0:T(8,128)(2,1)} fusion(bf16[1,6144,2560]{2,1,0:T(8,128)(2,1)} %bitcast.4, s32[3072]{0:T(1024)S(1)} %reshape.200), kind=kCustom, calls=%fused_computation | custom fusion | bytes 31481856 | tf_op jit(solution)/shard_map/vmap(jit(_take))/gather | solution.py:10
  450.6 27.2 %reshape.206 = f32[1,1,512,6,2560]{4,3,2,1,0:T(8,128)} reshape(bf16[3072,2560]{1,0:T(8,128)(2,1)} %gather_fusion) | data formatting | bytes 47185920 | tf_op jit(solution)/shard_map/convert_element_type | solution.py:15
  477.8 54.1 %multiply_reduce_fusion = f32[512,2560]{1,0:T(8,128)S(1)} fusion(f32[1,1,512,6,2560]{4,3,2,1,0:T(8,128)} %reshape.206, f32[512,6]{1,0:T(8,128)S(1)} %bitcast.87), kind=kLoop, calls=%fused_computation.2 | loop fusion | flops 14417920 | bytes 36712448 | tf_op jit(solution)/shard_map/reduce_sum | solution.py:15
  531.9 2.3 fusion.18
  534.2 1.2 collective-permute-start
  535.5 0.1 iota_compare_fusion
  535.6 58.4 %collective-permute-done = bf16[1,1,512,2560]{3,2,1,0:T(8,128)(2,1)S(1)} collective-permute-done((bf16[1,1,512,2560]{3,2,1,0:T(8,128)(2,1)}, bf16[1,1,512,2560]{3,2,1,0:T(8,128)(2,1)S(1)}, u32[]{:S(2)}, u32[]{:S(2)}) %collective-permute-start) | collective-permute-done | bytes 2621472 | tf_op jit(solution)/shard_map/ppermute | solution.py:62
  593.9 0.6 fusion.14
  594.5 11.2 %fusion.27 = bf16[512,2560]{1,0:T(8,128)(2,1)} fusion(bf16[1,2560,2560]{2,1,0:T(8,128)(2,1)} %param.17, bf16[1,1,512,2560]{3,2,1,0:T(8,128)(2,1)S(1)} %collective-permute-done, f32[2560]{0:T(1024)S(1)} %reduce.6, f32[512]{0:T(512)S(1)} %add_rsqrt_fusion), kind=kOutput, calls=%fused_computation.31 | convolution fusion | flops 6717440000 | bytes 18362368 | tf_op jit(solution)/shard_map/mbld,de->mble/dot_general | solution.py:28
  605.7 4.4 copy.42
  610.1 11.1 %fusion.24 = bf16[512,2560]{1,0:T(8,128)(2,1)} fusion(bf16[1,2560,2560]{2,1,0:T(8,128)(2,1)} %param.16, bf16[1,1,512,2560]{3,2,1,0:T(8,128)(2,1)S(1)} %collective-permute-done, f32[2560]{0:T(1024)S(1)} %reduce.6, f32[512]{0:T(512)S(1)} %add_rsqrt_fusion), kind=kOutput, calls=%fused_computation.30 | convolution fusion | flops 6717440000 | bytes 18362368 | tf_op jit(solution)/shard_map/mbld,de->mble/dot_general | solution.py:28
  621.2 4.5 copy.41
  625.7 11.1 %fusion.21 = bf16[512,2560]{1,0:T(8,128)(2,1)} fusion(bf16[1,2560,2560]{2,1,0:T(8,128)(2,1)} %param.18, bf16[1,1,512,2560]{3,2,1,0:T(8,128)(2,1)S(1)} %collective-permute-done, f32[2560]{0:T(1024)S(1)} %reduce.6, f32[512]{0:T(512)S(1)} %add_rsqrt_fusion), kind=kOutput, calls=%fused_computation.29 | convolution fusion | flops 6717440000 | bytes 18362368 | tf_op jit(solution)/shard_map/mbld,de->mble/dot_general | solution.py:28
  636.8 4.4 copy.40
  641.3 13.2 %fusion.53 = (f32[20,512]{1,0:T(8,128)S(1)}, f32[20,512,512]{1,2,0:T(8,128)}) fusion(pred[512,512]{0,1:T(8,128)(4,1)S(1)} %iota_compare_fusion, bf16[512,20,128]{0,2,1:T(8,128)(2,1)} %bitcast.85, bf16[512,20,128]{0,2,1:T(8,128)(2,1)} %bitcast.84), kind=kOutput, calls=%fused_computation.52 | convolution fusion | flops 1363149312 | bytes 26517504 | tf_op jit(solution)/shard_map/sub | solution.py:36
  654.4 9.3 %fusion.12 = bf16[20,128,512]{2,1,0:T(8,128)(2,1)S(1)} fusion(bf16[512,20,128]{0,2,1:T(8,128)(2,1)} %bitcast.86, f32[20,512,512]{1,2,0:T(8,128)} %get-tuple-element.6, f32[20,512]{1,0:T(8,128)S(1)} %get-tuple-element.5), kind=kOutput, calls=%fused_computation.17 | convolution fusion | flops 1352663040 | bytes 26255360 | tf_op jit(solution)/shard_map/mbhqk,mbkhe->mbqhe/dot_general | solution.py:37
  663.8 11.3 %fusion.35 = bf16[1,1,1,512,2560]{4,3,2,1,0:T(8,128)(2,1)} fusion(bf16[1,20,128,2560]{3,2,1,0:T(8,128)(2,1)} %param.19, bf16[1,1,512,2560]{3,2,1,0:T(8,128)(2,1)S(1)} %collective-permute-done, bf16[20,128,512]{2,1,0:T(8,128)(2,1)S(1)} %fusion.12), kind=kOutput, calls=%fused_computation.33 | convolution fusion | flops 6717440000 | bytes 20971520 | tf_op jit(solution)/shard_map/mbqhe,hed->mbqd/dot_general | solution.py:38
  (15 shorter events, 0.2 us)
Async XLA Ops:
  21.7 9.0 %copy-start.1 = (s32[1,1,1,512,6]{3,2,4,1,0:T(1,128)S(1)}, s32[1,1,1,512,6]{3,2,4,1,0:T(1,128)}, u32[]{:S(2)}) copy-start(s32[1,1,1,512,6]{3,2,4,1,0:T(1,128)} %param.12) | copy-start | bytes 36868
  21.7 9.0 %copy-start.2 = (s32[1,1,1,512,6]{3,2,4,1,0:T(1,128)S(1)}, s32[1,1,1,512,6]{3,2,4,1,0:T(1,128)}, u32[]{:S(2)}) copy-start(s32[1,1,1,512,6]{3,2,4,1,0:T(1,128)} %param.11) | copy-start | bytes 36868
  21.7 9.5 %copy-start.3 = (f32[1,1,1,512,6]{3,2,4,1,0:T(1,128)S(1)}, f32[1,1,1,512,6]{3,2,4,1,0:T(1,128)}, u32[]{:S(2)}) copy-start(f32[1,1,1,512,6]{3,2,4,1,0:T(1,128)} %param.13) | copy-start | bytes 36868
  21.7 349.8 %all-to-all-start = ((bf16[1,8,8,96,2560]{4,3,1,0,2:T(8,128)(2,1)}), bf16[1,8,8,96,2560]{4,3,1,0,2:T(8,128)(2,1)}, u32[]{:S(2)}, u32[]{:S(2)}) async-start(bf16[1,8,8,96,2560]{4,3,1,0,2:T(8,128)(2,1)} %copy.37), calls=%async_computation | async-start | bytes 62914560 | tf_op jit(solution)/shard_map/all_to_all | solution.py:54
  477.8 54.1 %copy-start = (bf16[1,1,1,512,2560]{4,3,2,1,0:T(8,128)(2,1)S(1)}, bf16[1,1,1,512,2560]{4,3,2,1,0:T(8,128)(2,1)}, u32[]{:S(2)}) copy-start(bf16[1,1,1,512,2560]{4,3,2,1,0:T(8,128)(2,1)} %param.14) | copy-start | bytes 7864324
  531.9 3.5 copy-start.4
  534.2 59.7 %collective-permute-start = (bf16[1,1,512,2560]{3,2,1,0:T(8,128)(2,1)}, bf16[1,1,512,2560]{3,2,1,0:T(8,128)(2,1)S(1)}, u32[]{:S(2)}, u32[]{:S(2)}) collective-permute-start(bf16[1,1,512,2560]{3,2,1,0:T(8,128)(2,1)} %fusion.18), channel_id=1, source_target_pairs={{0,8},{8,16},{16,24},{24,0},{1,9},{9,17},{17,25},{25,1},{2,10},{10... | collective-permute-start | bytes 7864328 | tf_op jit(solution)/shard_map/ppermute | solution.py:62
where the time goes:
time: 678 us; the launch traced here: 675 us
  waiting for transfers between devices  399 us (59%)
  local copies, waits for them, and re-layouts  142 us (21%)
  matrix products  67.3 us (10%)
  other arithmetic  57.2 us (8%)
  starting transfers between devices  10.2 us (2%)
    all_to_all x1, waiting for transfers between devices, local_step(): received = lax.all_to_all(split_view, 'ep', 2, 1, tiled=True)  340 us
    gather x3, local copies, waits for them, and re-layouts, take_rows(): return jnp.take(row_table, flat_ids, axis=0, mode='clip')  79.3 us
    ppermute x1, waiting for transfers between devices, local_step(): arrived = lax.ppermute(combined, 'pp', shift_pairs)  58.4 us
    reduce_sum x1, other arithmetic, combine_rows(): mixed = jnp.sum(gathered.astype(jnp.float32) * weights[..., None], axis=3)  54.1 us
    dot_general x3, matrix products, project(): jnp.einsum('mbld,de->mble', normed, w_mat, preferred_element_type=jnp.flo...  33.5 us
    convert_element_type x1, local copies, waits for them, and re-layouts, combine_rows(): mixed = jnp.sum(gathered.astype(jnp.float32) * weights[..., None], axis=3)  27.2 us
    another operation x1, local copies, waits for them, and re-layouts, local_step(): own_out.reshape(micro_count, local_experts, ep_size, slot_dev, model_dim)  21.7 us
  transfers between devices with their start and end apart: 2, of which 2 were waited for; matrix products, arithmetic and copies ran while one was open for 0% of the time, Pallas kernels for 0%

commit v1 on v0

v1 whole, which is shorter than its diff:
```python
import functools

import jax
import jax.numpy as jnp
from jax import lax
from jax.experimental import pallas as pl
from jax.experimental.pallas import tpu as pltpu
from jax.sharding import PartitionSpec as P

NORM_EPS = 1e-6
CORES = 2
CHUNK = 128
MESH = pl.DeviceIdType.MESH
F32 = jnp.float32
BF16 = jnp.bfloat16


def combine_kernel(dims, meta_ref, eo_ref, h_ref, out_ref, obuf, metas, mt, wbuf, part, own, recv, ybuf,
                   o_loc, o_send, o_recv, m_send, m_recv, r_send, r_recv, y_send, y_recv):
    ring, stages, experts, slot_dev, width, seq_len, top_k = dims
    half = width // 2
    depth = CORES * experts * slot_dev
    chunks = seq_len // CHUNK
    col_tile = 256
    tiles = half // col_tile
    ep = lax.axis_index('ep')
    stage = lax.axis_index('pp')
    chip = ep // CORES
    core = ep % CORES
    other = 1 - core

    def chip_at(offset):
        return lax.rem(chip + offset + ring, ring)

    def ep_at(offset):
        return {'ep': chip_at(offset) * CORES + core}

    partner = {'ep': chip * CORES + other}
    next_stage = {'pp': lax.rem(stage + 1, stages)}
    prev_stage = {'pp': lax.rem(stage + stages - 1, stages)}
    offsets = (-1, 1, 2, 0)

    barrier = pltpu.get_barrier_semaphore()
    peers = (partner, ep_at(-1), ep_at(1), ep_at(2), next_stage, prev_stage)
    for peer in peers:
        pl.semaphore_signal(barrier, inc=1, device_id=peer, device_id_type=MESH)
    pl.semaphore_wait(barrier, len(peers))

    def own_rows(slot, side):
        rows = pl.ds((chip_at(offsets[slot]) * CORES + core) * slot_dev, slot_dev)
        return pltpu.make_async_copy(eo_ref.at[:, rows, pl.ds(side * half, half)], obuf.at[slot, side, core],
                                     o_loc.at[slot, side])

    def partner_rows(slot, side):
        rows = pl.ds((chip_at(offsets[slot]) * CORES + other) * slot_dev, slot_dev)
        return pltpu.make_async_remote_copy(
            src_ref=eo_ref.at[:, rows, pl.ds(side * half, half)], dst_ref=obuf.at[slot, side, core],
            send_sem=o_send.at[slot, side], recv_sem=o_recv.at[slot, side], device_id=partner, device_id_type=MESH)

    meta_copies = [pltpu.make_async_remote_copy(
        src_ref=meta_ref, dst_ref=metas.at[slot], send_sem=m_send.at[slot], recv_sem=m_recv.at[slot],
        device_id=ep_at(-offsets[slot]), device_id_type=MESH) for slot in range(3)]
    for copy in meta_copies:
        copy.start()
    order = ((0, 0), (1, 1), (0, 1), (1, 0), (2, 0), (2, 1), (3, 0), (3, 1))
    for slot, side in order:
        partner_rows(slot, side).start()
        own_rows(slot, side).start()

    ready = set()

    def need_rows(slot, side):
        if (slot, side) not in ready:
            ready.add((slot, side))
            own_rows(slot, side).wait()
            partner_rows(slot, side).wait_recv()

    def need_meta(slot):
        if slot < 3 and slot not in ready:
            ready.add(slot)
            meta_copies[slot].wait_recv()

    base = (chip * depth).astype(F32)
    lane = lax.broadcasted_iota(jnp.int32, (16, 128), 1).astype(F32) + base

    def build(bank, slot, q):
        need_meta(slot)
        cols = slice(q * CHUNK, (q + 1) * CHUNK)
        block = meta_ref[:, cols] if slot == 3 else metas[slot, :, cols]
        mt[...] = jnp.transpose(block)

        def rows_step(step, carry):
            at = pl.multiple_of(step * 16, 16)
            rows = mt[pl.ds(at, 16), :]
            keys = [jnp.broadcast_to(rows[:, k:k + 1], (16, 128)) for k in range(top_k)]
            gates = [jnp.broadcast_to(rows[:, 8 + k:9 + k], (16, 128)) for k in range(top_k)]
            for tile in range(depth // 128):
                place = lane + float(tile * 128)
                weight = jnp.zeros((16, 128), F32)
                for k in range(top_k):
                    weight = jnp.where(keys[k] == place, gates[k], weight)
                high = weight.astype(BF16)
                rest = weight - high.astype(F32)
                mid = rest.astype(BF16)
                low = (rest - mid.astype(F32)).astype(BF16)
                at_col = slice(tile * 128, (tile + 1) * 128)
                wbuf[bank, pl.ds(at, 16), at_col] = high
                wbuf[bank, pl.ds(CHUNK + at, 16), at_col] = mid
                wbuf[bank, pl.ds(2 * CHUNK + at, 16), at_col] = low
            return carry

        lax.fori_loop(0, CHUNK // 16, rows_step, 0)

    def product(bank, slot, side, tile):
        at = pl.multiple_of(tile * col_tile, col_tile)
        rows = obuf[slot, side, :, :, :, pl.ds(at, col_tile)].reshape(depth, col_tile)
        res = jnp.dot(wbuf[bank], rows, preferred_element_type=F32)
        return at, (res[2 * CHUNK:] + res[CHUNK:2 * CHUNK]) + res[:CHUNK]

    def weigh(bank, slot, side, dst):
        need_rows(slot, side)

        def step(tile, carry):
            at, value = product(bank, slot, side, tile)
            dst[:, pl.ds(at, col_tile)] = value
            return carry

        lax.fori_loop(0, tiles, step, 0)

    def ring_copy(q, step, way):
        src = part.at[q % 2, way, way] if step == 0 else recv.at[q, step - 1, way]
        return pltpu.make_async_remote_copy(
            src_ref=src, dst_ref=recv.at[q, step, way], send_sem=r_send.at[q, step, way], recv_sem=r_recv.at[q, step, way],
            device_id=ep_at(1 if way == 0 else -1), device_id_type=MESH)

    def add_part(q, step, way, slot):
        def rows_step(i, carry):
            at = pl.ds(pl.multiple_of(i * 16, 16), 16)
            recv[q, step, way, at, :] = recv[q, step, way, at, :] + part[q % 2, slot, way, at, :]
            return carry

        lax.fori_loop(0, CHUNK // 16, rows_step, 0)

    def stage_a(q):
        par = q % 2
        if q >= 2:
            for way in (0, 1):
                ring_copy(q - 2, 0, way).wait_send()
        build(0, 0, q)
        weigh(0, 0, 0, part.at[par, 0, 0])
        ring_copy(q, 0, 0).start()
        build(1, 1, q)
        weigh(1, 1, 1, part.at[par, 1, 1])
        ring_copy(q, 0, 1).start()
        weigh(0, 0, 1, part.at[par, 0, 1])
        weigh(1, 1, 0, part.at[par, 1, 0])

    def stage_b(q):
        build(0, 2, q)
        for way in (0, 1):
            weigh(0, 2, way, part.at[q % 2, 2, way])
        for way in (0, 1):
            ring_copy(q, 0, way).wait_recv()
            add_part(q, 0, way, 2)
            ring_copy(q, 1, way).start()

    def stage_c(q):
        for way in (0, 1):
            ring_copy(q, 1, way).wait_recv()
            add_part(q, 1, way, 1 - way)
            ring_copy(q, 2, way).start()

    def y_copy(q):
        rows = pl.ds(q * CHUNK, CHUNK)
        return pltpu.make_async_remote_copy(
            src_ref=ybuf.at[q], dst_ref=out_ref.at[rows, :], send_sem=y_send.at[q], recv_sem=y_recv.at[q],
            device_id=next_stage, device_id_type=MESH)

    def stage_d(q):
        build(0, 3, q)
        for way in (0, 1):
            weigh(0, 3, way, own.at[way])
        for way in (0, 1):
            ring_copy(q, 2, way).wait_recv()

            def rows_step(i, carry, way=way):
                at = pl.multiple_of(i * 16, 16)
                total = h_ref[pl.ds(q * CHUNK + at, 16), way * half:(way + 1) * half].astype(F32)
                total = total + (recv[q, 2, way, pl.ds(at, 16), :] + own[way, pl.ds(at, 16), :])
                ybuf[q, pl.ds(at, 16), way * half:(way + 1) * half] = total.astype(BF16)
                return carry

            lax.fori_loop(0, CHUNK // 16, rows_step, 0)
        y_copy(q).start()

    for first in range(0, chunks, 2):
        if first == 0:
            stage_a(0)
            stage_a(1)
        stage_b(first)
        stage_b(first + 1)
        stage_c(first)
        if first + 2 < chunks:
            stage_a(first + 2)
        stage_c(first + 1)
        if first + 3 < chunks:
            stage_a(first + 3)
        stage_d(first)
        stage_d(first + 1)

    for copy in meta_copies:
        copy.wait_send()
    for slot, side in order:
        partner_rows(slot, side).wait_send()
    for q in range(chunks):
        for way in (0, 1):
            for step in range(3):
                if step > 0 or q >= chunks - 2:
                    ring_copy(q, step, way).wait_send()
        y_copy(q).wait()


def combine_call(meta, expert_out, resid, ring, stages):
    experts, capacity, width = expert_out.shape
    seq_len = resid.shape[0]
    slot_dev = capacity // (ring * CORES)
    half = width // 2
    depth = CORES * experts * slot_dev
    chunks = seq_len // CHUNK
    top_k = 6
    dims = (ring, stages, experts, slot_dev, width, seq_len, top_k)
    dma = pltpu.SemaphoreType.DMA
    return pl.pallas_call(
        functools.partial(combine_kernel, dims),
        out_shape=jax.ShapeDtypeStruct((seq_len, width), BF16),
        in_specs=[pl.BlockSpec(memory_space=pltpu.VMEM), pl.BlockSpec(memory_space=pl.ANY),
                  pl.BlockSpec(memory_space=pltpu.VMEM)],
        out_specs=pl.BlockSpec(memory_space=pl.ANY),
        scratch_shapes=[
            pltpu.VMEM((4, 2, CORES, experts, slot_dev, half), BF16),
            pltpu.VMEM((3, 16, seq_len), F32),
            pltpu.VMEM((CHUNK, 16), F32),
            pltpu.VMEM((2, 3 * CHUNK, depth), BF16),
            pltpu.VMEM((2, 3, 2, CHUNK, half), F32),
            pltpu.VMEM((2, CHUNK, half), F32),
            pltpu.VMEM((chunks, 3, 2, CHUNK, half), F32),
            pltpu.VMEM((chunks, CHUNK, width), BF16),
            dma((4, 2)), dma((4, 2)), dma((4, 2)),
            dma((3,)), dma((3,)),
            dma((chunks, 3, 2)), dma((chunks, 3, 2)),
            dma((chunks,)), dma((chunks,)),
        ],
        compiler_params=pltpu.CompilerParams(collective_id=0, has_side_effects=True, vmem_limit_bytes=67_000_000),
        name='combine',
    )(meta, expert_out, resid)


def attend_kernel(head_dim, y_ref, gain_ref, wq_ref, wk_ref, wv_ref, wo_ref, z_ref, x_ref, acc_ref, ctx_ref):
    step = pl.program_id(0)
    last = pl.num_programs(0) - 1
    seq_len, width = y_ref.shape
    group = wq_ref.shape[1]
    block = 128

    @pl.when(step == 0)
    def _():
        def rows_step(i, carry):
            at = pl.ds(pl.multiple_of(i * 16, 16), 16)
            x = y_ref[at, :].astype(F32)
            inv_rms = lax.rsqrt(jnp.mean(x * x, axis=-1, keepdims=True) + NORM_EPS)
            x_ref[at, :] = (x * inv_rms * gain_ref[...]).astype(BF16)
            return carry

        lax.fori_loop(0, seq_len // 16, rows_step, 0)

    x = x_ref[...]
    q = jnp.dot(x, wq_ref[...], preferred_element_type=F32).astype(BF16)
    k = jnp.dot(x, wk_ref[...], preferred_element_type=F32).astype(BF16)
    v = jnp.dot(x, wv_ref[...], preferred_element_type=F32).astype(BF16)
    row = lax.broadcasted_iota(jnp.int32, (block, block), 0)
    col = lax.broadcasted_iota(jnp.int32, (block, block), 1)
    keep = row >= col
    for head in range(group // head_dim):
        lanes = slice(head * head_dim, (head + 1) * head_dim)
        for qb in range(seq_len // block):
            rows = slice(qb * block, (qb + 1) * block)
            seen = (qb + 1) * block
            s = lax.dot_general(q[rows, lanes], k[:seen, lanes], (((1,), (1,)), ((), ())),
                                preferred_element_type=F32) * head_dim ** -0.5
            diag = jnp.where(keep, s[:, qb * block:], -jnp.inf)
            s = diag if qb == 0 else jnp.concatenate([s[:, :qb * block], diag], axis=1)
            e = jnp.exp(s - jnp.max(s, axis=-1, keepdims=True))
            p = (e / jnp.sum(e, axis=-1, keepdims=True)).astype(BF16)
            ctx_ref[rows, lanes] = jnp.dot(p, v[:seen, lanes], preferred_element_type=F32).astype(BF16)

    ctx = ctx_ref[...]
    tile = 512

    @pl.when(step == 0)
    def _():
        for n in range(width // tile):
            cols = slice(n * tile, (n + 1) * tile)
            acc_ref[:, cols] = jnp.dot(ctx, wo_ref[:, cols], preferred_element_type=F32)

    @pl.when(step > 0)
    def _():
        for n in range(width // tile):
            cols = slice(n * tile, (n + 1) * tile)
            acc_ref[:, cols] += jnp.dot(ctx, wo_ref[:, cols], preferred_element_type=F32)

    @pl.when(step == last)
    def _():
        def rows_step(i, carry):
            at = pl.ds(pl.multiple_of(i * 16, 16), 16)
            proj = acc_ref[at, :].astype(BF16).astype(F32)
            z_ref[at, :] = (y_ref[at, :].astype(F32) + proj).astype(BF16)
            return carry

        lax.fori_loop(0, seq_len // 16, rows_step, 0)


def attend_call(arrived, gain, w_query, w_key, w_value, w_out, head_dim):
    seq_len, width = arrived.shape
    hidden = w_query.shape[1]
    group = 2 * head_dim
    whole = lambda i: (0, 0)
    in_col = pl.BlockSpec((width, group), lambda i: (0, i))
    return pl.pallas_call(
        functools.partial(attend_kernel, head_dim),
        grid=(hidden // group,),
        out_shape=jax.ShapeDtypeStruct((seq_len, width), BF16),
        in_specs=[pl.BlockSpec((seq_len, width), whole), pl.BlockSpec((1, width), whole), in_col, in_col, in_col,
                  pl.BlockSpec((group, width), lambda i: (i, 0))],
        out_specs=pl.BlockSpec((seq_len, width), whole),
        scratch_shapes=[pltpu.VMEM((seq_len, width), BF16), pltpu.VMEM((seq_len, width), F32),
                        pltpu.VMEM((seq_len, group), BF16)],
        compiler_params=pltpu.CompilerParams(vmem_limit_bytes=60_000_000),
        name='attend',
    )(arrived, gain, w_query, w_key, w_value, w_out)


def solution(mesh):
    stages = mesh.shape['pp']
    ep_size = mesh.shape['ep']
    ring = ep_size // CORES
    assert ring == 4
    token_spec = P(('data', 'pp'), None, 'ep', None, None)
    weight_spec = P('pp', None, None)

    def local_step(expert_out, expert_ids, slot_ids, gates, resid, norm_scale, w_query, w_key, w_value, w_out):
        experts, capacity, width = expert_out.shape[2:]
        slot_dev = capacity // ep_size
        ids, slots, gate = expert_ids[0, 0, 0], slot_ids[0, 0, 0], gates[0, 0, 0]
        keys = jnp.where(slots >= 0, ids * slot_dev + slots - lax.axis_index('ep') * slot_dev, -1).astype(F32)
        pad = ((0, 8 - keys.shape[1]), (0, 0))
        meta = jnp.concatenate([jnp.pad(keys.T, pad), jnp.pad(gate.T, pad)], axis=0)
        arrived = combine_call(meta, expert_out[0, 0], resid[0, 0, 0], ring, stages)
        heads, head_dim = w_out.shape[1:3]
        z = attend_call(arrived, norm_scale, w_query[0], w_key[0], w_value[0],
                        w_out[0].reshape(heads * head_dim, width), head_dim)
        return z[None, None, None]

    return jax.shard_map(local_step, mesh=mesh, in_specs=(token_spec, token_spec, token_spec, token_spec, token_spec, P('pp', None), weight_spec, weight_spec, weight_spec, P('pp', None, None, None)), out_specs=token_spec, check_vma=False)
```

time: 678 us -> 278 us (0.41)
  waiting for transfers between devices: 399 us -> 0 us
  Pallas kernels: 0 us -> 275 us
  local copies, waits for them, and re-layouts: 142 us -> 0.71 us
  matrix products: 67.3 us -> 0 us
  other arithmetic: 57.2 us -> 1.35 us
  starting transfers between devices: 10.2 us -> 0 us
    all_to_all x1 -> x0, waiting for transfers between devices: 340 us -> none  [local_step(): received = lax.all_to_all(split_view, 'ep', 2, 1, tiled=True)]
    pallas_call x0 -> x2, Pallas kernels: none -> 275 us  [the longest x1 204 us: combine_call(): pl.pallas_call(functools.partial(combine_kernel, dims), out_shape=jax.Sha...]
    gather x3 -> x0, local copies, waits for them, and re-layouts: 79.3 us -> none  [take_rows(): return jnp.take(row_table, flat_ids, axis=0, mode='clip')]
    ppermute x1 -> x0, waiting for transfers between devices: 58.4 us -> none  [local_step(): arrived = lax.ppermute(combined, 'pp', shift_pairs)]
    reduce_sum x2 -> x0, other arithmetic: 54.7 us -> none  [the longest x1 54.1 us: combine_rows(): mixed = jnp.sum(gathered.astype(jnp.float32) * weights[..., None], axis=3)]
    dot_general x5 -> x0, matrix products: 54.1 us -> none  [the longest x3 33.5 us: project(): jnp.einsum('mbld,de->mble', normed, w_mat, preferred_element_type=jnp.flo...]
    convert_element_type x4 -> x0, local copies, waits for them, and re-layouts: 40.5 us -> none  [the longest x1 27.2 us: combine_rows(): mixed = jnp.sum(gathered.astype(jnp.float32) * weights[..., None], axis=3)]
    another operation x1 -> x0, local copies, waits for them, and re-layouts: 21.7 us -> none  [local_step(): own_out.reshape(micro_count, local_experts, ep_size, slot_dev, model_dim)]
  transfers between devices with their start and end apart: 2 -> 0, of which waited for: 2 -> 0; matrix products, arithmetic and copies ran while one was open for 0% -> 0% of each run, Pallas kernels for 0% -> 0%
where the time goes in v1:
time: 278 us; the launch traced here: 277 us
  Pallas kernels  275 us (99%)
    pallas_call x1, Pallas kernels, combine_call(): pl.pallas_call(functools.partial(combine_kernel, dims), out_shape=jax.Sha...  204 us
    pallas_call x1, Pallas kernels, attend_call(): pl.pallas_call(functools.partial(attend_kernel, head_dim), grid=(hidden /...  71.4 us

profile of v1, /device:TPU:97, one launch (start us, length us, event | category | flops | bytes accessed | tf_op | source)
XLA Modules:
  0.0 277.5 jit_solution(13801219194810273514)
XLA Ops:
  0.0 0.7 fusion.3
  0.7 0.7 copy.31
  1.4 0.6 select_maximum_fusion.meta_ref
  2.1 204.0 %combine.1.y_ref = bf16[512,2560]{1,0:T(8,128)(2,1)} custom-call(f32[16,512]{1,0:T(8,128)} %select_maximum_fusion.meta_ref, bf16[8,768,2560]{2,1,0:T(8,128)(2,1)} %bitcast.16, bf16[512,2560]{1,0:T(8,128)(2,1)} %bitcast.21), custom_call_target="tpu_custom_call" | custom-call | tf_op jit(solution)/shard_map/combine/pallas_call | solution.py:233
  206.1 71.4 %attend.1 = bf16[512,2560]{1,0:T(8,128)(2,1)} custom-call(bf16[512,2560]{1,0:T(8,128)(2,1)} %combine.1.y_ref, f32[1,2560]{1,0:T(1,128)} %gain_ref.1, bf16[2560,2560]{1,0:T(8,128)(2,1)} %bitcast.17, bf16[2560,2560]{1,0:T(8,128)(2,1)} %bitcast.18, bf16[2560,2560]{1,0:T(8,128)(2,1)} %bitcast.19, bf16[2560,2560]{1,0:T(8,128)(2,1)} %bitcast.20), custom_call_target="tpu_custom_call" | custom-call | tf_op jit(solution)/shard_map/attend/pallas_call | solution.py:328

commit v2 on v0

v2 whole, which is shorter than its diff:
```python
import functools

import jax
import jax.numpy as jnp
from jax import lax
from jax.experimental import pallas as pl
from jax.experimental.pallas import tpu as pltpu
from jax.sharding import PartitionSpec as P

NORM_EPS = 1e-6
CORES = 2
SIZES = (160, 144, 128, 80)
MESH = pl.DeviceIdType.MESH
F32 = jnp.float32
BF16 = jnp.bfloat16
LANES = 128
COLS = 256
DEEP = 3


def fused_kernel(dims, meta_ref, gain_ref, eo_ref, h_ref, wq_ref, wk_ref, wv_ref, wo_ref, z_ref, prow,
                 obuf, metas, mt, wbuf, part, recv, ybuf, yrecv, hbuf, wtile, kc, vc, xs, ctx, zbuf,
                 b_sem, o_send, o_recv, m_send, m_recv, r_send, r_recv, y_send, y_recv, h_sem, w_sem, z_sem):
    ring, stages, experts, slot_dev, width, seq_len, top_k, head_dim = dims
    half = width // 2
    depth = CORES * experts * slot_dev
    starts = [sum(SIZES[:q]) for q in range(len(SIZES))]
    chunks = len(SIZES)
    ep = lax.axis_index('ep')
    stage = lax.axis_index('pp')
    chip = ep // CORES
    core = ep % CORES
    other = 1 - core

    def chip_at(offset):
        return lax.rem(chip + offset + ring, ring)

    def ep_at(offset):
        return {'ep': chip_at(offset) * CORES + core}

    partner = {'ep': chip * CORES + other}
    next_stage = {'pp': lax.rem(stage + 1, stages)}
    prev_stage = {'pp': lax.rem(stage + stages - 1, stages)}
    offsets = (-1, 1, 2, 0)

    barrier = pltpu.get_barrier_semaphore()
    peers = (partner, ep_at(-1), ep_at(1), ep_at(2), next_stage, prev_stage)
    for peer in peers:
        pl.semaphore_signal(barrier, inc=1, device_id=peer, device_id_type=MESH)
    pl.semaphore_wait(barrier, len(peers))

    def partner_rows(slot, side):
        rows = pl.ds((chip_at(offsets[slot]) * CORES + other) * slot_dev, slot_dev)
        return pltpu.make_async_remote_copy(
            src_ref=eo_ref.at[:, rows, pl.ds(side * half, half)], dst_ref=prow.at[slot, side],
            send_sem=o_send.at[slot, side], recv_sem=o_recv.at[slot, side], device_id=partner, device_id_type=MESH)

    meta_copies = [pltpu.make_async_remote_copy(
        src_ref=meta_ref, dst_ref=metas.at[slot], send_sem=m_send.at[slot], recv_sem=m_recv.at[slot],
        device_id=ep_at(-offsets[slot]), device_id_type=MESH) for slot in range(3)]
    first_blocks = ((2, 0), (2, 1), (1, 1), (0, 0), (1, 0), (0, 1))
    own_blocks = ((3, 0), (3, 1))
    for copy in meta_copies:
        copy.start()
    for slot, side in first_blocks + own_blocks:
        partner_rows(slot, side).start()

    uses = list(first_blocks) + list(own_blocks) + list(first_blocks) * 2 + list(own_blocks) + list(first_blocks) \
        + list(own_blocks) * 2
    arrived = set()

    def block_copies(index):
        slot, side = uses[index]
        buf = index % 2
        rows = pl.ds((chip_at(offsets[slot]) * CORES + core) * slot_dev, slot_dev)
        mine = pltpu.make_async_copy(eo_ref.at[:, rows, pl.ds(side * half, half)], obuf.at[buf, core], b_sem.at[buf, 0])
        theirs = pltpu.make_async_copy(prow.at[slot, side], obuf.at[buf, other], b_sem.at[buf, 1])
        return mine, theirs

    def fetch_block(index):
        if index < len(uses):
            mine, theirs = block_copies(index)
            mine.start()
            if uses[index] not in arrived:
                arrived.add(uses[index])
                partner_rows(*uses[index]).wait_recv()
            theirs.start()

    pairs = width // COLS
    outs = pairs // 2
    steps = pairs + outs

    def qkv_copies(step, buf):
        cols = pl.ds(pl.multiple_of(step * COLS, COLS), COLS)
        return [pltpu.make_async_copy(ref.at[:, cols], wtile.at[buf, i], w_sem.at[buf, i])
                for i, ref in enumerate((wq_ref, wk_ref, wv_ref))]

    def out_copies(step, buf):
        return [pltpu.make_async_copy(wo_ref.at[:, pl.ds(pl.multiple_of(step * 2 * COLS + i * COLS, COLS), COLS)],
                                      wtile.at[buf, i], w_sem.at[buf, i]) for i in range(2)]

    def start_all(copies):
        for copy in copies:
            copy.start()

    fetch_block(0)
    for step in range(DEEP - 1):
        start_all(qkv_copies(step, step))

    def zero_step(i, carry):
        at = pl.ds(pl.multiple_of(i * 16, 16), 16)
        kc[at, :] = jnp.zeros((16, width), BF16)
        vc[at, :] = jnp.zeros((16, width), BF16)
        return carry

    lax.fori_loop(0, seq_len // 16, zero_step, 0)

    base = (chip * depth).astype(F32)
    lane = lax.broadcasted_iota(jnp.int32, (16, LANES), 1).astype(F32) + base
    met = set()

    def build(bank, slot, q):
        if slot < 3 and slot not in met:
            met.add(slot)
            meta_copies[slot].wait_recv()
        size = SIZES[q]
        for lo in range(0, seq_len, LANES):
            if lo < starts[q] + size and lo + LANES > starts[q]:
                cols = slice(lo, lo + LANES)
                block = meta_ref[:, cols] if slot == 3 else metas[slot, :, cols]
                mt[lo:lo + LANES, :] = jnp.transpose(block)

        def rows_step(step, carry):
            at = pl.multiple_of(step * 16, 16)
            rows = mt[pl.ds(starts[q] + at, 16), :]
            keys = [jnp.broadcast_to(rows[:, k:k + 1], (16, LANES)) for k in range(top_k)]
            gates = [jnp.broadcast_to(rows[:, 8 + k:9 + k], (16, LANES)) for k in range(top_k)]
            for tile in range(depth // LANES):
                place = lane + float(tile * LANES)
                weight = jnp.zeros((16, LANES), F32)
                for k in range(top_k):
                    weight = jnp.where(keys[k] == place, gates[k], weight)
                high = weight.astype(BF16)
                rest = weight - high.astype(F32)
                mid = rest.astype(BF16)
                low = (rest - mid.astype(F32)).astype(BF16)
                at_col = slice(tile * LANES, (tile + 1) * LANES)
                wbuf[bank, pl.ds(at, 16), at_col] = high
                wbuf[bank, pl.ds(size + at, 16), at_col] = mid
                wbuf[bank, pl.ds(2 * size + at, 16), at_col] = low
            return carry

        lax.fori_loop(0, size // 16, rows_step, 0)

    used = [0]

    def weigh(bank, slot, side, q, dst):
        index = used[0]
        used[0] += 1
        assert uses[index] == (slot, side)
        size = SIZES[q]
        buf = index % 2
        fetch_block(index + 1)
        for copy in block_copies(index):
            copy.wait()

        def step(tile, carry):
            at = pl.multiple_of(tile * COLS, COLS)
            rows = obuf[buf, :, :, :, pl.ds(at, COLS)].reshape(depth, COLS)
            res = jnp.dot(wbuf[bank, :3 * size], rows, preferred_element_type=F32)
            dst[:size, pl.ds(at, COLS)] = (res[2 * size:] + res[size:2 * size]) + res[:size]
            return carry

        lax.fori_loop(0, half // COLS, step, 0)

    sent = (((2, 0), (2, 1)), ((1, 1), (0, 0)), ((1, 0), (0, 1)))

    def ring_copy(q, kind, way):
        slot, side = sent[kind][way]
        rows = pl.ds(starts[q], SIZES[q])
        return pltpu.make_async_remote_copy(
            src_ref=part.at[q % 2, slot, side, pl.ds(0, SIZES[q])], dst_ref=recv.at[kind, way, rows],
            send_sem=r_send.at[q, kind, way], recv_sem=r_recv.at[q, kind, way],
            device_id=ep_at(1 if way == 0 else -1), device_id_type=MESH)

    def residual(q):
        return pltpu.make_async_copy(h_ref.at[pl.ds(starts[q], SIZES[q])], hbuf.at[pl.ds(0, SIZES[q])], h_sem)

    def partials(q):
        par = part.at[q % 2]
        if q >= 2:
            for way in (0, 1):
                ring_copy(q - 2, 1, way).wait_send()
                ring_copy(q - 2, 2, way).wait_send()
        build(0, 2, q)
        weigh(0, 2, 0, q, par.at[2, 0])
        ring_copy(q, 0, 0).start()
        weigh(0, 2, 1, q, par.at[2, 1])
        ring_copy(q, 0, 1).start()
        build(1, 1, q)
        weigh(1, 1, 1, q, par.at[1, 1])
        ring_copy(q, 1, 0).start()
        build(0, 0, q)
        weigh(0, 0, 0, q, par.at[0, 0])
        ring_copy(q, 1, 1).start()
        weigh(1, 1, 0, q, par.at[1, 0])
        weigh(0, 0, 1, q, par.at[0, 1])

    def pass_on(q):
        for way in (0, 1):
            slot, side = sent[2][way]
            ring_copy(q, 0, way).wait_recv()

            def rows_step(i, carry, way=way, slot=slot, side=side):
                at = pl.multiple_of(i * 16, 16)
                mine = part[q % 2, slot, side, pl.ds(at, 16), :]
                part[q % 2, slot, side, pl.ds(at, 16), :] = mine + recv[0, way, pl.ds(starts[q] + at, 16), :]
                return carry

            lax.fori_loop(0, SIZES[q] // 16, rows_step, 0)
            ring_copy(q, 2, way).start()

    def own_partials(q):
        for way in (0, 1):
            ring_copy(q, 0, way).wait_send()
        build(0, 3, q)
        for side in (0, 1):
            weigh(0, 3, side, q, part.at[q % 2, 2, side])

    def y_copy(q):
        return pltpu.make_async_remote_copy(
            src_ref=ybuf.at[pl.ds(starts[q], SIZES[q])], dst_ref=yrecv.at[pl.ds(starts[q], SIZES[q])],
            send_sem=y_send.at[q], recv_sem=y_recv.at[q], device_id=next_stage, device_id_type=MESH)

    def finish(q):
        residual(q).wait()
        for way in (0, 1):
            ring_copy(q, 1, way).wait_recv()
            ring_copy(q, 2, way).wait_recv()
        for side in (0, 1):

            def rows_step(i, carry, side=side):
                at = pl.multiple_of(i * 16, 16)
                rows = pl.ds(starts[q] + at, 16)
                cols = slice(side * half, (side + 1) * half)
                total = part[q % 2, 2, side, pl.ds(at, 16), :]
                total = total + recv[1, 1 - side, rows, :]
                total = total + recv[2, side, rows, :]
                total = total + hbuf[pl.ds(at, 16), cols].astype(F32)
                ybuf[rows, cols] = total.astype(BF16)
                return carry

            lax.fori_loop(0, SIZES[q] // 16, rows_step, 0)
        y_copy(q).start()
        if q + 1 < chunks:
            residual(q + 1).start()

    def z_copy(q):
        return pltpu.make_async_copy(zbuf.at[pl.ds(0, SIZES[q])], z_ref.at[pl.ds(starts[q], SIZES[q])], z_sem)

    def attend(q, between=None):
        size, start = SIZES[q], starts[q]
        seen = -(-(start + size) // LANES) * LANES
        y_copy(q).wait_recv()

        def norm_step(i, carry):
            at = pl.multiple_of(i * 16, 16)
            x = yrecv[pl.ds(start + at, 16), :].astype(F32)
            inv_rms = lax.rsqrt(jnp.mean(x * x, axis=-1, keepdims=True) + NORM_EPS)
            xs[pl.ds(at, 16), :] = (x * inv_rms * gain_ref[...]).astype(BF16)
            return carry

        lax.fori_loop(0, size // 16, norm_step, 0)
        row = lax.broadcasted_iota(jnp.int32, (size, seen), 0) + start
        col = lax.broadcasted_iota(jnp.int32, (size, seen), 1)

        def head_step(step, carry):
            buf = lax.rem(step, DEEP)
            ahead = lax.rem(step + DEEP - 1, DEEP)

            @pl.when(step + DEEP - 1 < pairs)
            def _():
                start_all(qkv_copies(step + DEEP - 1, ahead))

            @pl.when(step + DEEP - 1 >= pairs)
            def _():
                start_all(out_copies(step + DEEP - 1 - pairs, ahead))

            for copy in qkv_copies(step, buf):
                copy.wait()
            x = xs[:size]
            lanes = pl.ds(pl.multiple_of(step * COLS, COLS), COLS)
            qh = jnp.dot(x, wtile[buf, 0], preferred_element_type=F32).astype(BF16)
            kc[pl.ds(start, size), lanes] = jnp.dot(x, wtile[buf, 1], preferred_element_type=F32).astype(BF16)
            vc[pl.ds(start, size), lanes] = jnp.dot(x, wtile[buf, 2], preferred_element_type=F32).astype(BF16)
            for head in range(COLS // head_dim):
                one = pl.ds(pl.multiple_of(step * COLS + head * head_dim, head_dim), head_dim)
                s = lax.dot_general(qh[:, head * head_dim:(head + 1) * head_dim], kc[:seen, one],
                                    (((1,), (1,)), ((), ())), preferred_element_type=F32) * head_dim ** -0.5
                s = jnp.where(row >= col, s, -jnp.inf)
                e = jnp.exp(s - jnp.max(s, axis=-1, keepdims=True))
                p = (e * (1.0 / jnp.sum(e, axis=-1, keepdims=True))).astype(BF16)
                ctx[:size, one] = jnp.dot(p, vc[:seen, one], preferred_element_type=F32).astype(BF16)
            return carry

        lax.fori_loop(0, pairs, head_step, 0)
        if between is not None:
            between()
        if q > 0:
            z_copy(q - 1).wait()

        def out_step(step, carry):
            index = step + pairs
            buf = lax.rem(index, DEEP)
            ahead = lax.rem(index + DEEP - 1, DEEP)

            @pl.when(step + DEEP - 1 < outs)
            def _():
                start_all(out_copies(step + DEEP - 1, ahead))

            if q + 1 < chunks:
                @pl.when(step + DEEP - 1 >= outs)
                def _():
                    start_all(qkv_copies(step + DEEP - 1 - outs, ahead))

            for copy in out_copies(step, buf):
                copy.wait()
            for i in range(2):
                lanes = pl.ds(pl.multiple_of(step * 2 * COLS + i * COLS, COLS), COLS)
                proj = jnp.dot(ctx[:size], wtile[buf, i], preferred_element_type=F32).astype(BF16).astype(F32)
                zbuf[:size, lanes] = (yrecv[pl.ds(start, size), lanes].astype(F32) + proj).astype(BF16)
            return carry

        lax.fori_loop(0, outs, out_step, 0)
        z_copy(q).start()

    residual(0).start()
    partials(0)
    pass_on(0)
    own_partials(0)
    partials(1)
    finish(0)
    for q in range(1, chunks):
        if q + 1 < chunks:
            partials(q + 1)
        pass_on(q)
        own_partials(q)
        if q < chunks - 1:
            attend(q - 1)
            finish(q)
        else:
            attend(q - 1, functools.partial(finish, q))
    attend(chunks - 1)

    z_copy(chunks - 1).wait()
    for copy in meta_copies:
        copy.wait_send()
    for slot, side in first_blocks + own_blocks:
        partner_rows(slot, side).wait_send()
    for q in range(chunks):
        y_copy(q).wait_send()
        for way in (0, 1):
            if q >= chunks - 2:
                ring_copy(q, 1, way).wait_send()
                ring_copy(q, 2, way).wait_send()


def fused_call(meta, gain, expert_out, resid, w_query, w_key, w_value, w_out, head_dim, ring, stages):
    experts, capacity, width = expert_out.shape
    seq_len = resid.shape[0]
    slot_dev = capacity // (ring * CORES)
    half = width // 2
    depth = CORES * experts * slot_dev
    chunks = len(SIZES)
    largest = max(SIZES)
    assert sum(SIZES) == seq_len and w_query.shape[1] == width
    dims = (ring, stages, experts, slot_dev, width, seq_len, 6, head_dim)
    dma = pltpu.SemaphoreType.DMA
    anywhere = pl.BlockSpec(memory_space=pl.ANY)
    local = pl.BlockSpec(memory_space=pltpu.VMEM)
    return pl.pallas_call(
        functools.partial(fused_kernel, dims),
        out_shape=[jax.ShapeDtypeStruct((seq_len, width), BF16),
                   jax.ShapeDtypeStruct((4, 2, experts, slot_dev, half), BF16)],
        in_specs=[local, local] + [anywhere] * 6,
        out_specs=[anywhere, anywhere],
        scratch_shapes=[
            pltpu.VMEM((2, CORES, experts, slot_dev, half), BF16),
            pltpu.VMEM((3, 16, seq_len), F32),
            pltpu.VMEM((seq_len, 16), F32),
            pltpu.VMEM((2, 3 * largest, depth), BF16),
            pltpu.VMEM((2, 3, 2, largest, half), F32),
            pltpu.VMEM((3, 2, seq_len, half), F32),
            pltpu.VMEM((seq_len, width), BF16),
            pltpu.VMEM((seq_len, width), BF16),
            pltpu.VMEM((largest, width), BF16),
            pltpu.VMEM((DEEP, 3, width, COLS), BF16),
            pltpu.VMEM((seq_len, width), BF16),
            pltpu.VMEM((seq_len, width), BF16),
            pltpu.VMEM((largest, width), BF16),
            pltpu.VMEM((largest, width), BF16),
            pltpu.VMEM((largest, width), BF16),
            dma((2, 2)), dma((4, 2)), dma((4, 2)),
            dma((3,)), dma((3,)),
            dma((chunks, 3, 2)), dma((chunks, 3, 2)),
            dma((chunks,)), dma((chunks,)),
            dma, dma((DEEP, 3)), dma,
        ],
        compiler_params=pltpu.CompilerParams(collective_id=0, has_side_effects=True, vmem_limit_bytes=67_043_328),
        name='combine_attend',
    )(meta, gain, expert_out, resid, w_query, w_key, w_value, w_out)[0]


def solution(mesh):
    stages = mesh.shape['pp']
    ep_size = mesh.shape['ep']
    ring = ep_size // CORES
    assert ring == 4
    token_spec = P(('data', 'pp'), None, 'ep', None, None)
    weight_spec = P('pp', None, None)

    def local_step(expert_out, expert_ids, slot_ids, gates, resid, norm_scale, w_query, w_key, w_value, w_out):
        experts, capacity, width = expert_out.shape[2:]
        slot_dev = capacity // ep_size
        ids, slots, gate = expert_ids[0, 0, 0], slot_ids[0, 0, 0], gates[0, 0, 0]
        keys = jnp.where(slots >= 0, ids * slot_dev + slots - lax.axis_index('ep') * slot_dev, -1).astype(F32)
        pad = ((0, 8 - keys.shape[1]), (0, 0))
        meta = jnp.concatenate([jnp.pad(keys.T, pad), jnp.pad(gate.T, pad)], axis=0)
        heads, head_dim = w_out.shape[1:3]
        z = fused_call(meta, norm_scale, expert_out[0, 0], resid[0, 0, 0], w_query[0], w_key[0], w_value[0],
                       w_out[0].reshape(heads * head_dim, width), head_dim, ring, stages)
        return z[None, None, None]

    return jax.shard_map(local_step, mesh=mesh, in_specs=(token_spec, token_spec, token_spec, token_spec, token_spec, P('pp', None), weight_spec, weight_spec, weight_spec, P('pp', None, None, None)), out_specs=token_spec, check_vma=False)
```

time: 678 us -> 262 us (0.39)
  waiting for transfers between devices: 399 us -> 0 us
  Pallas kernels: 0 us -> 256 us
  local copies, waits for them, and re-layouts: 142 us -> 4.11 us
  matrix products: 67.3 us -> 0 us
  other arithmetic: 57.2 us -> 1.35 us
  starting transfers between devices: 10.2 us -> 0 us
    all_to_all x1 -> x0, waiting for transfers between devices: 340 us -> none  [local_step(): received = lax.all_to_all(split_view, 'ep', 2, 1, tiled=True)]
    pallas_call x0 -> x1, Pallas kernels: none -> 256 us  [fused_call(): pl.pallas_call(functools.partial(fused_kernel, dims), out_shape=[jax.Shap...]
    gather x3 -> x0, local copies, waits for them, and re-layouts: 79.3 us -> none  [take_rows(): return jnp.take(row_table, flat_ids, axis=0, mode='clip')]
    ppermute x1 -> x0, waiting for transfers between devices: 58.4 us -> none  [local_step(): arrived = lax.ppermute(combined, 'pp', shift_pairs)]
    reduce_sum x2 -> x0, other arithmetic: 54.7 us -> none  [the longest x1 54.1 us: combine_rows(): mixed = jnp.sum(gathered.astype(jnp.float32) * weights[..., None], axis=3)]
    dot_general x5 -> x0, matrix products: 54.1 us -> none  [the longest x3 33.5 us: project(): jnp.einsum('mbld,de->mble', normed, w_mat, preferred_element_type=jnp.flo...]
    convert_element_type x4 -> x0, local copies, waits for them, and re-layouts: 40.5 us -> none  [the longest x1 27.2 us: combine_rows(): mixed = jnp.sum(gathered.astype(jnp.float32) * weights[..., None], axis=3)]
    another operation x1 -> x0, local copies, waits for them, and re-layouts: 21.7 us -> none  [local_step(): own_out.reshape(micro_count, local_experts, ep_size, slot_dev, model_dim)]
  transfers between devices with their start and end apart: 2 -> 0, of which waited for: 2 -> 0; matrix products, arithmetic and copies ran while one was open for 0% -> 0% of each run, Pallas kernels for 0% -> 0%
where the time goes in v2:
time: 262 us; the launch traced here: 261 us
  Pallas kernels  256 us (98%)
  local copies, waits for them, and re-layouts  4.11 us (2%)
    pallas_call x1, Pallas kernels, fused_call(): pl.pallas_call(functools.partial(fused_kernel, dims), out_shape=[jax.Shap...  256 us

profile of v2, /device:TPU:97, one launch (start us, length us, event | category | flops | bytes accessed | tf_op | source)
XLA Modules:
  0.0 261.3 jit_solution(168506407037937876)
XLA Ops:
  0.0 0.7 fusion.3
  0.7 0.7 copy.31
  1.4 0.6 select_maximum_fusion.meta_ref
  2.1 255.8 %combine_attend.1 = (bf16[512,2560]{1,0:T(8,128)(2,1)}, bf16[4,2,8,96,1280]{4,3,2,1,0:T(8,128)(2,1)}) custom-call(f32[16,512]{1,0:T(8,128)} %select_maximum_fusion.meta_ref, f32[1,2560]{1,0:T(1,128)} %gain_ref.1, bf16[8,768,2560]{2,1,0:T(8,128)(2,1)} %bitcast.16, bf16[512,2560]{1,0:T(8,128)(2,1)} %bitcast.21, bf16[2560,2560]{1,0:T(8,128)(2,1)} %bitcast.17, ...), custom_call_target="tpu_custom_call" | custom-call | tf_op jit(solution)/shard_map/combine_attend/pallas_call | solution.py:381
  257.9 3.4 %copy.33 = bf16[1,1,1,512,2560]{4,3,2,1,0:T(8,128)(2,1)} copy(bf16[1,1,1,512,2560]{4,3,2,1,0:T(8,128)(2,1)} %bitcast.22) | data formatting | bytes 5242880

commit v3 on v2

--- a/solution.py
+++ b/solution.py
@@ -10,6 +10,7 @@
 NORM_EPS = 1e-6
 CORES = 2
 SIZES = (160, 144, 128, 80)
+HOOK = 4
 MESH = pl.DeviceIdType.MESH
 F32 = jnp.float32
 BF16 = jnp.bfloat16
@@ -186,7 +187,7 @@
     def residual(q):
         return pltpu.make_async_copy(h_ref.at[pl.ds(starts[q], SIZES[q])], hbuf.at[pl.ds(0, SIZES[q])], h_sem)
 
-    def partials(q):
+    def partials(q, send):
         par = part.at[q % 2]
         if q >= 2:
             for way in (0, 1):
@@ -194,17 +195,26 @@
                 ring_copy(q - 2, 2, way).wait_send()
         build(0, 2, q)
         weigh(0, 2, 0, q, par.at[2, 0])
-        ring_copy(q, 0, 0).start()
+        if send:
+            ring_copy(q, 0, 0).start()
         weigh(0, 2, 1, q, par.at[2, 1])
-        ring_copy(q, 0, 1).start()
+        if send:
+            ring_copy(q, 0, 1).start()
         build(1, 1, q)
         weigh(1, 1, 1, q, par.at[1, 1])
-        ring_copy(q, 1, 0).start()
+        if send:
+            ring_copy(q, 1, 0).start()
         build(0, 0, q)
         weigh(0, 0, 0, q, par.at[0, 0])
-        ring_copy(q, 1, 1).start()
+        if send:
+            ring_copy(q, 1, 1).start()
         weigh(1, 1, 0, q, par.at[1, 0])
         weigh(0, 0, 1, q, par.at[0, 1])
+
+    def send_partials(q):
+        for kind in (0, 1):
+            for way in (0, 1):
+                ring_copy(q, kind, way).start()
 
     def pass_on(q):
         for way in (0, 1):
@@ -303,9 +313,12 @@
                 ctx[:size, one] = jnp.dot(p, vc[:seen, one], preferred_element_type=F32).astype(BF16)
             return carry
 
-        lax.fori_loop(0, pairs, head_step, 0)
-        if between is not None:
+        if between is None:
+            lax.fori_loop(0, pairs, head_step, 0)
+        else:
+            lax.fori_loop(0, HOOK, head_step, 0)
             between()
+            lax.fori_loop(HOOK, pairs, head_step, 0)
         if q > 0:
             z_copy(q - 1).wait()
 
@@ -335,15 +348,17 @@
         z_copy(q).start()
 
     residual(0).start()
-    partials(0)
+    partials(0, True)
     pass_on(0)
     own_partials(0)
-    partials(1)
+    partials(1, True)
     finish(0)
     for q in range(1, chunks):
         if q + 1 < chunks:
-            partials(q + 1)
+            partials(q + 1, False)
         pass_on(q)
+        if q + 1 < chunks:
+            send_partials(q + 1)
         own_partials(q)
         if q < chunks - 1:
             attend(q - 1)

time: 262 us -> 231 us (0.88)
  Pallas kernels: 256 us -> 225 us
    pallas_call x1, Pallas kernels: 256 us -> 225 us  [fused_call(): pl.pallas_call(functools.partial(fused_kernel, dims), out_shape=[jax.Shap...]
where the time goes in v3:
time: 231 us
  Pallas kernels  225 us (97%)
  local copies, waits for them, and re-layouts  4.11 us (2%)
    pallas_call x1, Pallas kernels, fused_call(): pl.pallas_call(functools.partial(fused_kernel, dims), out_shape=[jax.Shap...  225 us

profile of v3, /device:TPU:97, one launch (start us, length us, event | category | flops | bytes accessed | tf_op | source)
XLA Modules:
  0.0 230.7 jit_solution(8445304581753778586)
XLA Ops:
  0.0 0.7 fusion.3
  0.7 0.7 copy.31
  1.4 0.6 select_maximum_fusion.meta_ref
  2.1 225.2 %combine_attend.1 = (bf16[512,2560]{1,0:T(8,128)(2,1)}, bf16[4,2,8,96,1280]{4,3,2,1,0:T(8,128)(2,1)}) custom-call(f32[16,512]{1,0:T(8,128)} %select_maximum_fusion.meta_ref, f32[1,2560]{1,0:T(1,128)} %gain_ref.1, bf16[8,768,2560]{2,1,0:T(8,128)(2,1)} %bitcast.16, bf16[512,2560]{1,0:T(8,128)(2,1)} %bitcast.21, bf16[2560,2560]{1,0:T(8,128)(2,1)} %bitcast.17, ...), custom_call_target="tpu_custom_call" | custom-call | tf_op jit(solution)/shard_map/combine_attend/pallas_call | solution.py:396
  227.3 3.4 %copy.33 = bf16[1,1,1,512,2560]{4,3,2,1,0:T(8,128)(2,1)} copy(bf16[1,1,1,512,2560]{4,3,2,1,0:T(8,128)(2,1)} %bitcast.22) | data formatting | bytes 5242880
